TPU v7x, 32 devices: a whole 2x2x4 slice. The times are simulated.
32 devices in a mesh: groups: 2 (over y), expert: 8 (over z, core), tensor: 2 (over x).
Axes of the slice: x: 2, y: 2, z: 4, core: 2. Of those that a mesh axis runs over, the one named last changes fastest.
Arguments:
- query: bfloat16 [768, 8192], P(('groups', 'expert'), 'tensor'), parts along dimension 0, may hold values from -40 to 40
- latest_key_value: bfloat16 [768, 2, 512], P(('groups', 'expert'), None, 'tensor'), parts along dimension 0, may hold values from -6 to 6
- cache: bfloat16 [768, 2, 128, 512], P(('groups', 'expert'), None, None, 'tensor'), parts along dimension 0, may hold values from -6 to 6
- lengths: int32 [768], P(('groups', 'expert')), parts along dimension 0, may hold values from 2 to 128
- w_out: bfloat16 [8192, 4096], P('tensor', 'expert'), may hold values from -0.0625 to 0.0625
- residual_in: bfloat16 [768, 4096], P(('groups', 'expert', 'tensor')), parts along dimension 0, may hold values from -6 to 6
- norm_gain: bfloat16 [4096], replicated, may hold values from 0.5 to 1.5
- expert_ids: int32 [768, 8], P(('groups', 'expert')), parts along dimension 0, may hold values from 0 to 15, all different within a row; in each aligned block of 48 rows (0 to 47, 48 to 95, ...) at most 48 rows name the same one
- route_weights: float32 [768, 8], P(('groups', 'expert')), parts along dimension 0, may hold values from 0.05 to 0.5
- w_gate: bfloat16 [16, 4096, 768], P('expert', None, 'tensor'), may hold values from -0.09375 to 0.09375
- w_up: bfloat16 [16, 4096, 768], P('expert', None, 'tensor'), may hold values from -0.09375 to 0.09375
- w_down: bfloat16 [16, 768, 4096], P('expert', 'tensor'), may hold values from -0.21875 to 0.21875
Outputs:
- layer_out: bfloat16 [768, 4096], P(('groups', 'expert', 'tensor')), parts along dimension 0
There are 2 independent parts, one for each index of `groups`. A program takes and returns all parts, laid end to end along the dimension named above; an argument that names none is the same for every part. Nothing has to cross between parts.
Inputs may be any that keep to these rules, and one draw needn't show every extreme that they name: `expert_ids`: the 8 entries of a row differ. Within each aligned block of 48 rows (the rows of one index of the expert axis) no expert is named by more than 48 rows, and in every draw some block reaches that bound.
All inputs are finite; a program needn't handle non-finite values.
Results may differ from a plain program's by a relative error of at most 0.0095.
Values may be sent and summed in bfloat16 or wider, within the bound.
A program may use at most 128 MiB of HBM per device.

v0:
```python
import math

import jax
import jax.numpy as jnp
from jax import lax
from jax.sharding import PartitionSpec as P

HEAD_SIZE = 128


def attention(query, latest_key_value, cache, lengths):
    token_count = query.shape[0]
    kv_heads = latest_key_value.shape[2] // HEAD_SIZE
    group_size = query.shape[1] // (kv_heads * HEAD_SIZE)
    positions = cache.shape[2]
    factor = 1.0 / math.sqrt(HEAD_SIZE)
    queries = query.reshape(token_count, kv_heads, group_size, HEAD_SIZE)
    cached_keys = cache[:, 0].reshape(token_count, positions, kv_heads, HEAD_SIZE)
    cached_values = cache[:, 1].reshape(token_count, positions, kv_heads, HEAD_SIZE)
    fresh_keys = latest_key_value[:, 0].reshape(token_count, kv_heads, HEAD_SIZE)
    fresh_values = (
        latest_key_value[:, 1].reshape(token_count, kv_heads, HEAD_SIZE).astype(jnp.float32)
    )
    scores = (
        jnp.einsum("tkgd,tlkd->tkgl", queries, cached_keys, preferred_element_type=jnp.float32)
        * factor
    )
    valid = jnp.arange(positions, dtype=jnp.int32)[None, :] < lengths[:, None]
    scores = jnp.where(valid[:, None, None, :], scores, -jnp.inf)
    own_score = (
        jnp.einsum("tkgd,tkd->tkg", queries, fresh_keys, preferred_element_type=jnp.float32)
        * factor
    )
    highest = jnp.maximum(jnp.max(scores, axis=-1), own_score)
    weights = jnp.exp(scores - highest[..., None])
    own_weight = jnp.exp(own_score - highest)
    total = jnp.sum(weights, axis=-1) + own_weight
    probs = (weights / total[..., None]).astype(jnp.bfloat16)
    own_prob = lax.optimization_barrier((own_weight / total).astype(jnp.bfloat16))
    mixed = jnp.einsum("tkgl,tlkd->tkgd", probs, cached_values, preferred_element_type=jnp.float32)
    mixed = mixed + own_prob.astype(jnp.float32)[..., None] * fresh_values[:, :, None, :]
    return mixed.reshape(token_count, -1).astype(jnp.bfloat16)


def per_device(
    query,
    latest_key_value,
    cache,
    lengths,
    w_out,
    residual_in,
    norm_gain,
    expert_ids,
    route_weights,
    w_gate,
    w_up,
    w_down,
):
    attended = attention(query, latest_key_value, cache, lengths)
    projected = jnp.dot(
        lax.all_gather(attended, "expert", axis=0, tiled=True),
        w_out,
        preferred_element_type=jnp.float32,
    )
    expert_groups = lax.axis_size("expert")
    token_count = query.shape[0]
    column_count = w_out.shape[1]
    grouped = projected.reshape(expert_groups, token_count, column_count)
    summed = lax.psum_scatter(
        grouped.astype(jnp.bfloat16), "tensor", scatter_dimension=1, tiled=True
    ).astype(jnp.float32)
    own_rows = lax.all_to_all(
        summed.astype(jnp.bfloat16), "expert", split_axis=0, concat_axis=2, tiled=True
    ).astype(summed.dtype)
    stream = residual_in.astype(jnp.float32) + own_rows.reshape(residual_in.shape)
    meansq = jnp.mean(stream * stream, axis=-1, keepdims=True)
    normed = (stream * lax.rsqrt(meansq + 1e-06) * norm_gain.astype(jnp.float32)).astype(
        jnp.bfloat16
    )
    choose_count = expert_ids.shape[1]
    local_experts = w_gate.shape[0]
    expert_total = local_experts * expert_groups
    capacity = min(token_count, 2 * token_count * choose_count // expert_total)
    slot_total = expert_total * capacity
    flat_ids = expert_ids.reshape(-1)
    onehot = (flat_ids[:, None] == jnp.arange(expert_total, dtype=jnp.int32)[None, :]).astype(
        jnp.int32
    )
    earlier = jnp.cumsum(onehot, axis=0) - onehot
    slot_index = jnp.sum(earlier * onehot, axis=1)
    target = (flat_ids * capacity + slot_index).reshape(token_count, choose_count)
    matches = target[:, :, None] == jnp.arange(slot_total, dtype=jnp.int32)[None, None, :]
    selector = jnp.any(matches, axis=1).astype(jnp.bfloat16)
    mixing = jnp.sum(jnp.where(matches, route_weights[:, :, None], 0.0), axis=1)
    contract = (((0,), (0,)), ((), ()))
    whole_rows = lax.all_gather(normed, "tensor", axis=0, tiled=True)
    packed = lax.dot_general(selector, whole_rows, contract, preferred_element_type=jnp.float32)
    packed = packed.astype(jnp.bfloat16).reshape(expert_total, capacity, -1)
    arrived = lax.all_to_all(packed, "expert", split_axis=0, concat_axis=1, tiled=True)
    gate_proj = jnp.einsum("xsd,xdf->xsf", arrived, w_gate, preferred_element_type=jnp.float32)
    up_proj = jnp.einsum("xsd,xdf->xsf", arrived, w_up, preferred_element_type=jnp.float32)
    activated = (jax.nn.silu(gate_proj) * up_proj).astype(jnp.bfloat16)
    partial_out = jnp.einsum("xsf,xfd->xsd", activated, w_down, preferred_element_type=jnp.float32)
    expert_out = lax.psum_scatter(
        partial_out.astype(jnp.bfloat16), "tensor", scatter_dimension=2, tiled=True
    )
    returned = lax.all_to_all(expert_out, "expert", split_axis=1, concat_axis=0, tiled=True)
    mixture = jnp.dot(
        mixing,
        returned.reshape(slot_total, -1).astype(jnp.float32),
        precision=lax.Precision.HIGHEST,
    )
    mixture_rows = lax.all_to_all(
        mixture.astype(jnp.bfloat16), "tensor", split_axis=0, concat_axis=1, tiled=True
    ).astype(mixture.dtype)
    return (stream + mixture_rows).astype(jnp.bfloat16)


def solution(mesh):
    placed = (
        P(("groups", "expert"), "tensor"),
        P(("groups", "expert"), None, "tensor"),
        P(("groups", "expert"), None, None, "tensor"),
        P(("groups", "expert")),
        P("tensor", "expert"),
        P(("groups", "expert", "tensor"), None),
        P(),
        P(("groups", "expert"), None),
        P(("groups", "expert"), None),
        P("expert", None, "tensor"),
        P("expert", None, "tensor"),
        P("expert", "tensor", None),
    )
    return jax.shard_map(
        per_device,
        mesh=mesh,
        in_specs=placed,
        out_specs=P(("groups", "expert", "tensor"), None),
        check_vma=False,
    )
```

profile of v0, /device:TPU:0, one launch (start us, length us, event | category | flops | bytes accessed | tf_op | source)
XLA Modules:
  0.0 453.0 jit_solution(3351646385357858465)
XLA Ops:
  6.5 6.3 %fusion.17 = (bf16[48,1,128,256]{3,2,1,0:T(8,128)(2,1)}, bf16[48,1,128,256]{3,2,1,0:T(8,128)(2,1)}) fusion(bf16[48,2,128,256]{3,2,1,0:T(8,128)(2,1)} %param.14), kind=kLoop, calls=%fused_computation.47 | loop fusion | bytes 12582912 | tf_op jit(solution)/shard_map/slice | solution.py:18
  12.8 3.5 copy.99
  16.5 0.9 slice_convert_fusion
  17.4 1.1 fusion.8
  18.5 1.1 fusion.18
  19.6 0.8 copy-done.1
  21.2 4.8 %copy.100 = bf16[48,1,128,256]{2,3,0,1:T(8,128)(2,1)} copy(bf16[48,1,128,256]{3,2,1,0:T(8,128)(2,1)} %get-tuple-element.6) | data formatting | bytes 6291456
  25.9 3.7 fusion.2
  29.6 0.9 copy.112
  30.6 41.0 %all-gather.2.cloned.1.call-done = bf16[384,4096]{1,0:T(8,128)(2,1)} async-done(((bf16[48,4096]{1,0:T(8,128)(2,1)}), bf16[384,4096]{1,0:T(8,128)(2,1)}) %all-gather.2.cloned.1.call-update) | async-done | bytes 3145744 | tf_op jit(solution)/shard_map/all_gather | solution.py:61
  71.6 4.9 %convolution_convert_fusion.3 = bf16[384,512]{1,0:T(8,128)(2,1)S(1)} fusion(bf16[384,4096]{1,0:T(8,128)(2,1)} %all-gather.2.cloned.1.call-done, bf16[4096,512]{1,0:T(8,128)(2,1)} %param.16), kind=kOutput, calls=%fused_computation.9 | convolution fusion | flops 1610809344 | bytes 7733248 | tf_op jit(solution)/shard_map/dot_general | solution.py:60
  76.6 0.8 copy.105
  77.7 0.9 reduce-window.6
  79.1 10.6 %reduce-scatter.7.cloned.1.call-done = bf16[24,4096]{1,0:T(8,128)(2,1)} async-done(((bf16[48,4096]{1,0:T(8,128)(2,1)}), bf16[24,4096]{1,0:T(8,128)(2,1)}) %reduce-scatter.7.cloned.1.call-update) | async-done | bytes 196624
  89.6 1.0 copy.106
  91.3 4.6 %all-to-all-start = ((bf16[8,24,512]{2,1,0:T(8,128)(2,1)}), bf16[8,24,512]{2,1,0:T(8,128)(2,1)S(1)}, u32[]{:S(2)}, u32[]{:S(2)}) async-start(bf16[8,24,512]{2,1,0:T(8,128)(2,1)} %copy.98), calls=%async_computation | async-start | bytes 393216 | tf_op jit(solution)/shard_map/all_to_all | solution.py:72
  96.7 7.6 %all-to-all-done = bf16[8,24,512]{2,1,0:T(8,128)(2,1)S(1)} async-done(((bf16[8,24,512]{2,1,0:T(8,128)(2,1)}), bf16[8,24,512]{2,1,0:T(8,128)(2,1)S(1)}, u32[]{:S(2)}, u32[]{:S(2)}) %all-to-all-start) | async-done | bytes 196640 | tf_op jit(solution)/shard_map/all_to_all | solution.py:72
  104.7 6.3 %all_gather.7 = bf16[48,4096]{1,0:T(8,128)(2,1)S(1)} all-gather(bf16[24,4096]{1,0:T(8,128)(2,1)S(1)} %multiply_convert_fusion), channel_id=1, replica_groups=mesh['groups'=2,'expert'=8,'tensor'=2] {'tensor'}, dimensions={0}, use_global_device_ids=true | all-gather | bytes 589824 | tf_op jit(solution)/shard_map/all_gather | solution.py:96
  111.0 1.8 convolution_convert_fusion
  112.9 142.7 %all_to_all.55 = bf16[16,48,4096]{2,1,0:T(8,128)(2,1)S(1)} all-to-all(bf16[16,48,4096]{2,1,0:T(8,128)(2,1)S(1)} %bitcast.89), channel_id=1, replica_groups=mesh['groups'=2,'expert'=8,'tensor'=2] {'expert'}, dimensions={0} | all-to-all | bytes 12582912 | tf_op jit(solution)/shard_map/all_to_all | solution.py:99
  255.6 0.8 copy.88
  256.4 2.7 copy-done
  259.1 4.5 fusion.20
  263.5 12.6 %convolution_convert_fusion.1 = bf16[2,384,4096]{2,1,0:T(8,128)(2,1)} fusion(bf16[2,384,4096]{2,1,0:T(8,128)(2,1)} %param.23, bf16[2,384,4096]{2,1,0:T(8,128)(2,1)} %bitcast.95, bf16[2,4096,384]{2,1,0:T(8,128)(2,1)} %param.22, f32[2,384,384]{2,1,0:T(8,128)} %fusion.20), kind=kOutput, calls=%fused_computation.1 | convolution fusion | flops 4836753408 | bytes 26345472 | tf_op jit(solution)/shard_map/xsf,xfd->xsd/dot_general | solution.py:103
  276.2 75.3 %reduce-scatter.5.cloned.1.call-done = bf16[2,384,2048]{2,1,0:T(8,128)(2,1)} async-done(((bf16[2,384,4096]{2,1,0:T(8,128)(2,1)}), bf16[2,384,2048]{2,1,0:T(8,128)(2,1)}) %reduce-scatter.5.cloned.1.call-update) | async-done | bytes 3145744 | tf_op jit(solution)/shard_map/reduce_scatter | solution.py:104
  351.4 6.8 %copy.89 = bf16[2,384,2048]{2,0,1:T(2,128)(2,1)} copy(bf16[2,384,2048]{2,1,0:T(8,128)(2,1)} %reduce-scatter.5.cloned.1.call-done) | data formatting | bytes 6291456 | tf_op jit(solution)/shard_map/reduce_scatter | solution.py:104
  358.2 4.7 %all-to-all-start.2 = ((bf16[2,384,2048]{2,0,1:T(2,128)(2,1)}), bf16[2,384,2048]{2,0,1:T(2,128)(2,1)S(1)}, u32[]{:S(2)}, u32[]{:S(2)}) async-start(bf16[2,384,2048]{2,0,1:T(2,128)(2,1)} %copy.89), calls=%async_computation.3 | async-start | bytes 6291456 | tf_op jit(solution)/shard_map/all_to_all | solution.py:107
  363.6 1.9 select_reduce_fusion
  365.5 69.0 %all-to-all-done.2 = bf16[2,384,2048]{2,0,1:T(2,128)(2,1)S(1)} async-done(((bf16[2,384,2048]{2,0,1:T(2,128)(2,1)}), bf16[2,384,2048]{2,0,1:T(2,128)(2,1)S(1)}, u32[]{:S(2)}, u32[]{:S(2)}) %all-to-all-start.2) | async-done | bytes 3145760 | tf_op jit(solution)/shard_map/all_to_all | solution.py:107
  434.5 1.4 copy.90
  436.7 1.7 convolution_convert_fusion.2
  438.5 7.2 %all_to_all.56 = bf16[2,24,2048]{2,1,0:T(8,128)(2,1)S(1)} all-to-all(bf16[2,24,2048]{2,1,0:T(8,128)(2,1)S(1)} %bitcast.106), channel_id=1, replica_groups=mesh['groups'=2,'expert'=8,'tensor'=2] {'tensor'}, dimensions={0} | all-to-all | bytes 393216 | tf_op jit(solution)/shard_map/all_to_all | solution.py:113
  (63 shorter events, 6.0 us)
Async XLA Ops:
  6.5 65.1 %all-gather.2.cloned.1.call-start = ((), (), s32[]{:S(2)}) async-start(), calls=%async_computation.6 | async-start | bytes 3538944 | tf_op jit(solution)/shard_map/all_gather | solution.py:61
  12.8 3.5 copy-start.6
  12.8 3.6 copy-start.11
  19.5 0.9 copy-start.1
  21.1 4.8 %copy-start.2 = (f32[48,2,16,128]{3,2,1,0:T(8,128)S(1)}, f32[48,2,16,128]{3,2,1,0:T(8,128)}, u32[]{:S(2)}) copy-start(f32[48,2,16,128]{3,2,1,0:T(8,128)} %copy-done.1) | copy-start | bytes 2359300
  30.5 46.8 %copy-start.8 = (s32[48,8]{0,1:T(8,128)S(1)}, s32[48,8]{0,1:T(8,128)}, u32[]{:S(2)}) copy-start(s32[48,8]{0,1:T(8,128)} %param.19) | copy-start | bytes 4612
  30.5 47.1 %copy-start.9 = (bf16[4096]{0:T(1024)(128)(2,1)S(1)}, bf16[4096]{0:T(1024)(128)(2,1)}, u32[]{:S(2)}) copy-start(bf16[4096]{0:T(1024)(128)(2,1)} %param.18) | copy-start | bytes 24580
  30.6 59.1 %reduce-scatter.7.cloned.1.call-start = ((), (), s32[]{:S(2)}) async-start(), calls=%async_computation.8 | async-start | bytes 589824
  76.6 27.8 %copy-start.3 = (bf16[24,4096]{1,0:T(8,128)(2,1)S(1)}, bf16[24,4096]{1,0:T(8,128)(2,1)}, u32[]{:S(2)}) copy-start(bf16[24,4096]{1,0:T(8,128)(2,1)} %param.17) | copy-start | bytes 589828
  91.3 12.9 %all-to-all-start = ((bf16[8,24,512]{2,1,0:T(8,128)(2,1)}), bf16[8,24,512]{2,1,0:T(8,128)(2,1)S(1)}, u32[]{:S(2)}, u32[]{:S(2)}) async-start(bf16[8,24,512]{2,1,0:T(8,128)(2,1)} %copy.98), calls=%async_computation | async-start | bytes 393216 | tf_op jit(solution)/shard_map/all_to_all | solution.py:72
  96.0 255.5 %reduce-scatter.5.cloned.1.call-start = ((), (), s32[]{:S(2)}) async-start(), calls=%async_computation.7 | async-start | bytes 9437184 | tf_op jit(solution)/shard_map/reduce_scatter | solution.py:104
  96.1 0.6 copy-start.7
  112.8 146.2 %slice-start = ((s8[6291456]{0:T(1024)(128)(4,1)}), s8[4194304]{0:T(1024)(128)(4,1)S(1)}, s32[]{:S(2)}) async-start(s8[6291456]{0:T(1024)(128)(4,1)} %bitcast.115), calls=%async_computation.9 | async-start | bytes 8388608
  255.6 3.5 slice-start.1
  256.4 2.7 copy-start
  358.2 4.7 %copy-start.10 = (f32[48,8]{0,1:T(8,128)S(1)}, f32[48,8]{0,1:T(8,128)}, u32[]{:S(2)}) copy-start(f32[48,8]{0,1:T(8,128)} %param.20) | copy-start | bytes 4612
  358.2 76.2 %all-to-all-start.2 = ((bf16[2,384,2048]{2,0,1:T(2,128)(2,1)}), bf16[2,384,2048]{2,0,1:T(2,128)(2,1)S(1)}, u32[]{:S(2)}, u32[]{:S(2)}) async-start(bf16[2,384,2048]{2,0,1:T(2,128)(2,1)} %copy.89), calls=%async_computation.3 | async-start | bytes 6291456 | tf_op jit(solution)/shard_map/all_to_all | solution.py:107
  435.8 0.9 copy-start.5
  436.3 9.5 %copy-start.4 = (bf16[24,4096]{1,0:T(8,128)(2,1)S(1)}, bf16[24,4096]{1,0:T(8,128)(2,1)}, u32[]{:S(2)}) copy-start(bf16[24,4096]{1,0:T(8,128)(2,1)} %param.17) | copy-start | bytes 589828
Sparse Core Ops, SparseCore 0:
  30.7 40.9 all-gather.1
  77.5 12.0 reduce-scatter.6
  276.3 75.0 reduce-scatter.4
where the time goes:
time: 454 us; the launch traced here: 453 us
  waiting for transfers between devices  203 us (45%)
  blocking collectives  156 us (34%)
  local copies, waits for them, and re-layouts  33 us (7%)
  matrix products  31.4 us (7%)
  between operations  13.4 us (3%)
  starting transfers between devices  9.44 us (2%)
  other arithmetic  6.05 us (1%)
    all_to_all x1, blocking collectives, per_device(): lax.all_to_all(packed, 'expert', split_axis=0, concat_axis=1, tiled=True)  143 us
    reduce_scatter x1, waiting for transfers between devices, per_device(): lax.psum_scatter(partial_out.astype(jnp.bfloat16), 'tensor', scatter_dime...  75.3 us
    all_to_all x1, waiting for transfers between devices, per_device(): lax.all_to_all(expert_out, 'expert', split_axis=1, concat_axis=0, tiled=T...  69 us
    all_gather x1, waiting for transfers between devices, per_device(): lax.all_gather(attended, 'expert', axis=0, tiled=True)  41 us
    unnamed x38, local copies, waits for them, and re-layouts  16.8 us
    dot_general x1, matrix products, per_device(): jnp.einsum('xsf,xfd->xsd', activated, w_down, preferred_element_type=jnp....  12.6 us
    unnamed x4, waiting for transfers between devices  10.6 us
  transfers between devices with their start and end apart: 5, of which 5 were waited for; matrix products, arithmetic and copies ran while one was open for 1% of the time, Pallas kernels for 0%

commit v1 on v0

--- a/solution.py
+++ b/solution.py
@@ -77,43 +77,33 @@
     normed = (stream * lax.rsqrt(meansq + 1e-06) * norm_gain.astype(jnp.float32)).astype(
         jnp.bfloat16
     )
-    choose_count = expert_ids.shape[1]
     local_experts = w_gate.shape[0]
     expert_total = local_experts * expert_groups
-    capacity = min(token_count, 2 * token_count * choose_count // expert_total)
-    slot_total = expert_total * capacity
-    flat_ids = expert_ids.reshape(-1)
-    onehot = (flat_ids[:, None] == jnp.arange(expert_total, dtype=jnp.int32)[None, :]).astype(
-        jnp.int32
+    named = expert_ids[:, :, None] == jnp.arange(expert_total, dtype=jnp.int32)[None, None, :]
+    mixing = jnp.sum(jnp.where(named, route_weights[:, :, None], 0.0), axis=1)
+    mixing = lax.all_to_all(
+        mixing.reshape(token_count, expert_groups, local_experts),
+        "expert",
+        split_axis=1,
+        concat_axis=0,
+        tiled=True,
+    ).reshape(token_count * expert_groups, local_experts)
+    whole_rows = lax.all_gather(normed, ("expert", "tensor"), axis=0, tiled=True)
+    pieces = []
+    for x in range(local_experts):
+        gate_proj = jnp.dot(whole_rows, w_gate[x], preferred_element_type=jnp.float32)
+        up_proj = jnp.dot(whole_rows, w_up[x], preferred_element_type=jnp.float32)
+        activated = jax.nn.silu(gate_proj) * up_proj * mixing[:, x][:, None]
+        pieces.append(activated.astype(jnp.bfloat16))
+    partial_out = jnp.dot(
+        jnp.concatenate(pieces, axis=1),
+        w_down.reshape(-1, w_down.shape[2]),
+        preferred_element_type=jnp.float32,
     )
-    earlier = jnp.cumsum(onehot, axis=0) - onehot
-    slot_index = jnp.sum(earlier * onehot, axis=1)
-    target = (flat_ids * capacity + slot_index).reshape(token_count, choose_count)
-    matches = target[:, :, None] == jnp.arange(slot_total, dtype=jnp.int32)[None, None, :]
-    selector = jnp.any(matches, axis=1).astype(jnp.bfloat16)
-    mixing = jnp.sum(jnp.where(matches, route_weights[:, :, None], 0.0), axis=1)
-    contract = (((0,), (0,)), ((), ()))
-    whole_rows = lax.all_gather(normed, "tensor", axis=0, tiled=True)
-    packed = lax.dot_general(selector, whole_rows, contract, preferred_element_type=jnp.float32)
-    packed = packed.astype(jnp.bfloat16).reshape(expert_total, capacity, -1)
-    arrived = lax.all_to_all(packed, "expert", split_axis=0, concat_axis=1, tiled=True)
-    gate_proj = jnp.einsum("xsd,xdf->xsf", arrived, w_gate, preferred_element_type=jnp.float32)
-    up_proj = jnp.einsum("xsd,xdf->xsf", arrived, w_up, preferred_element_type=jnp.float32)
-    activated = (jax.nn.silu(gate_proj) * up_proj).astype(jnp.bfloat16)
-    partial_out = jnp.einsum("xsf,xfd->xsd", activated, w_down, preferred_element_type=jnp.float32)
-    expert_out = lax.psum_scatter(
-        partial_out.astype(jnp.bfloat16), "tensor", scatter_dimension=2, tiled=True
+    mixture_rows = lax.psum_scatter(
+        partial_out.astype(jnp.bfloat16), ("expert", "tensor"), scatter_dimension=0, tiled=True
     )
-    returned = lax.all_to_all(expert_out, "expert", split_axis=1, concat_axis=0, tiled=True)
-    mixture = jnp.dot(
-        mixing,
-        returned.reshape(slot_total, -1).astype(jnp.float32),
-        precision=lax.Precision.HIGHEST,
-    )
-    mixture_rows = lax.all_to_all(
-        mixture.astype(jnp.bfloat16), "tensor", split_axis=0, concat_axis=1, tiled=True
-    ).astype(mixture.dtype)
-    return (stream + mixture_rows).astype(jnp.bfloat16)
+    return (stream + mixture_rows.astype(jnp.float32)).astype(jnp.bfloat16)
 
 
 def solution(mesh):

time: 454 us -> 239 us (0.53)
  blocking collectives: 156 us -> 7.98 us
  waiting for transfers between devices: 203 us -> 162 us
  local copies, waits for them, and re-layouts: 33 us -> 19 us
  starting transfers between devices: 9.44 us -> 4.74 us
    all_to_all x2 -> x1, blocking collectives: 150 us -> 7.98 us  [per_device(): lax.all_to_all(mixing.reshape(token_count, expert_groups, local_experts),...]
    all_to_all x1 -> x0, waiting for transfers between devices: 69 us -> none  [per_device(): lax.all_to_all(expert_out, 'expert', split_axis=1, concat_axis=0, tiled=T...]
    all_gather x0 -> x1, waiting for transfers between devices: none -> 35.4 us  [per_device(): lax.all_gather(normed, ('expert', 'tensor'), axis=0, tiled=True)]
    reduce_scatter x1, waiting for transfers between devices: 75.3 us -> 64.8 us  [per_device(): lax.psum_scatter(partial_out.astype(jnp.bfloat16), ('expert', 'tensor'),...]
    reduce_scatter x1 -> x0, local copies, waits for them, and re-layouts: 6.79 us -> none  [per_device(): lax.psum_scatter(partial_out.astype(jnp.bfloat16), 'tensor', scatter_dime...]
    all_gather x1 -> x0, blocking collectives: 6.34 us -> none  [per_device(): whole_rows = lax.all_gather(normed, 'tensor', axis=0, tiled=True)]
    all_to_all x1 -> x0, starting transfers between devices: 4.74 us -> none  [per_device(): lax.all_to_all(expert_out, 'expert', split_axis=1, concat_axis=0, tiled=T...]
    dot_general x4 -> x5, matrix products: 20.6 us -> 16.5 us  [the longest x2 8.73 us: per_device(): jnp.dot(whole_rows, w_gate[x], preferred_element_type=jnp.float32)]
  transfers between devices with their start and end apart: 5 -> 5, of which waited for: 5 -> 5; matrix products, arithmetic and copies ran while one was open for 1% -> 0% of each run, Pallas kernels for 0% -> 0%
where the time goes in v1:
time: 239 us
  waiting for transfers between devices  162 us (68%)
  matrix products  27.3 us (11%)
  local copies, waits for them, and re-layouts  19 us (8%)
  between operations  13.4 us (6%)
  blocking collectives  7.98 us (3%)
  starting transfers between devices  4.74 us (2%)
  other arithmetic  4.33 us (2%)
    reduce_scatter x1, waiting for transfers between devices, per_device(): lax.psum_scatter(partial_out.astype(jnp.bfloat16), ('expert', 'tensor'),...  64.8 us
    all_gather x1, waiting for transfers between devices, per_device(): lax.all_gather(attended, 'expert', axis=0, tiled=True)  41 us
    all_gather x1, waiting for transfers between devices, per_device(): lax.all_gather(normed, ('expert', 'tensor'), axis=0, tiled=True)  35.4 us
    unnamed x34, local copies, waits for them, and re-layouts  12.7 us
    unnamed x5, waiting for transfers between devices  12.3 us
    dot_general x2, matrix products, per_device(): jnp.dot(whole_rows, w_gate[x], preferred_element_type=jnp.float32)  8.73 us
    all_to_all x1, waiting for transfers between devices, per_device(): lax.all_to_all(summed.astype(jnp.bfloat16), 'expert', split_axis=0, conca...  8.24 us
    all_to_all x1, blocking collectives, per_device(): lax.all_to_all(mixing.reshape(token_count, expert_groups, local_experts),...  7.98 us
  transfers between devices with their start and end apart: 5, of which 5 were waited for; matrix products, arithmetic and copies ran while one was open for 0% of the time, Pallas kernels for 0%

profile of v1, /device:TPU:0, one launch (start us, length us, event | category | flops | bytes accessed | tf_op | source)
XLA Modules:
  0.0 238.6 jit_solution(4585028827960191101)
XLA Ops:
  6.5 6.2 %fusion.43 = (bf16[48,1,128,256]{3,2,1,0:T(8,128)(2,1)}, bf16[48,1,128,256]{3,2,1,0:T(8,128)(2,1)}) fusion(bf16[48,2,128,256]{3,2,1,0:T(8,128)(2,1)} %param.14), kind=kLoop, calls=%fused_computation.53 | loop fusion | bytes 12582912 | tf_op jit(solution)/shard_map/slice | solution.py:18
  12.8 3.5 %copy.44 = bf16[48,1,128,256]{2,3,0,1:T(8,128)(2,1)S(1)} copy(bf16[48,1,128,256]{3,2,1,0:T(8,128)(2,1)} %get-tuple-element.7) | data formatting | bytes 6291456
  16.4 0.1 iota_compare_fusion.1
  16.5 0.9 slice_convert_fusion
  17.3 1.1 fusion.38
  18.4 1.1 fusion.44
  19.6 0.9 copy-done
  20.4 0.6 fusion.32
  21.0 0.1 fusion.42
  21.1 4.7 %copy.45 = bf16[48,1,128,256]{2,3,0,1:T(8,128)(2,1)} copy(bf16[48,1,128,256]{3,2,1,0:T(8,128)(2,1)} %get-tuple-element.8) | data formatting | bytes 6291456
  25.9 3.7 %fusion.13 = bf16[48,2,16,128]{3,2,1,0:T(8,128)(2,1)S(1)} fusion(bf16[48,128,2,128]{1,3,2,0:T(8,128)(2,1)} %bitcast.91, f32[48,2,16,128]{3,2,1,0:T(8,128)S(1)} %copy-done.1, f32[48,2,128]{2,1,0:T(2,128)S(1)} %bitcast.103, f32[48,2,16]{2,1,0:T(2,128)S(1)} %convert_element_type.75, f32[48,2,16]{2,1,0:T(2,128)S(1)} %get-tuple-element.9, ...), kind=kOutput, calls=%fused_computation.16 | convolution fusion | flops 51511296 | bytes 4392960 | tf_op jit(solution)/shard_map/tkgl,tlkd->tkgd/dot_general | solution.py:40
  29.5 0.9 copy.54
  30.5 41.0 %all-gather.3.cloned.1.call-done = bf16[384,4096]{1,0:T(8,128)(2,1)} async-done(((bf16[48,4096]{1,0:T(8,128)(2,1)}), bf16[384,4096]{1,0:T(8,128)(2,1)}) %all-gather.3.cloned.1.call-update) | async-done | bytes 3145744 | tf_op jit(solution)/shard_map/all_gather | solution.py:61
  71.6 4.9 %convolution_convert_fusion.1 = bf16[384,512]{1,0:T(8,128)(2,1)S(1)} fusion(bf16[384,4096]{1,0:T(8,128)(2,1)} %all-gather.3.cloned.1.call-done, bf16[4096,512]{1,0:T(8,128)(2,1)} %param.16), kind=kOutput, calls=%fused_computation.21 | convolution fusion | flops 1610809344 | bytes 7733248 | tf_op jit(solution)/shard_map/dot_general | solution.py:60
  76.5 0.8 copy.48
  77.3 12.2 %reduce-scatter.7.cloned.1.call-done = bf16[24,4096]{1,0:T(8,128)(2,1)} async-done(((bf16[48,4096]{1,0:T(8,128)(2,1)}), bf16[24,4096]{1,0:T(8,128)(2,1)}) %reduce-scatter.7.cloned.1.call-update) | async-done | bytes 196624
  89.6 1.0 copy.49
  90.6 0.7 copy.43
  91.3 4.6 %all-to-all-start = ((bf16[8,24,512]{2,1,0:T(8,128)(2,1)}), bf16[8,24,512]{2,1,0:T(8,128)(2,1)S(1)}, u32[]{:S(2)}, u32[]{:S(2)}) async-start(bf16[8,24,512]{2,1,0:T(8,128)(2,1)} %copy.43), calls=%async_computation | async-start | bytes 393216 | tf_op jit(solution)/shard_map/all_to_all | solution.py:72
  96.0 8.2 %all-to-all-done = bf16[8,24,512]{2,1,0:T(8,128)(2,1)S(1)} async-done(((bf16[8,24,512]{2,1,0:T(8,128)(2,1)}), bf16[8,24,512]{2,1,0:T(8,128)(2,1)S(1)}, u32[]{:S(2)}, u32[]{:S(2)}) %all-to-all-start) | async-done | bytes 196640 | tf_op jit(solution)/shard_map/all_to_all | solution.py:72
  104.3 0.2 multiply_reduce_fusion
  104.5 0.8 multiply_convert_fusion
  105.4 8.0 %all_to_all.24 = f32[48,8,2]{0,2,1:T(2,128)S(1)} all-to-all(f32[48,8,2]{0,2,1:T(2,128)S(1)} %bitcast.105), channel_id=1, replica_groups=mesh['groups'=2,'expert'=8,'tensor'=2] {'expert'}, dimensions={1} | all-to-all | bytes 6144 | tf_op jit(solution)/shard_map/all_to_all | solution.py:84
  113.4 0.1 reshape.66
  113.5 35.4 %all-gather.5.cloned.1.call-done = bf16[384,4096]{1,0:T(8,128)(2,1)} async-done(((bf16[24,4096]{1,0:T(8,128)(2,1)}), bf16[384,4096]{1,0:T(8,128)(2,1)}) %all-gather.5.cloned.1.call-update) | async-done | bytes 3145744 | tf_op jit(solution)/shard_map/all_gather | solution.py:91
  148.9 4.8 %fusion.6 = f32[384,384]{0,1:T(8,128)S(1)} fusion(bf16[384,4096]{1,0:T(8,128)(2,1)} %all-gather.5.cloned.1.call-done, bf16[2,4096,384]{2,1,0:T(8,128)(2,1)} %param.21), kind=kOutput, calls=%fused_computation.7 | convolution fusion | flops 1207959552 | bytes 6881280 | tf_op jit(solution)/shard_map/dot_general | solution.py:94
  153.7 3.9 %fusion.2 = f32[384,384]{0,1:T(8,128)S(1)} fusion(bf16[384,4096]{1,0:T(8,128)(2,1)S(1)} %copy-done.8, bf16[2,4096,384]{2,1,0:T(8,128)(2,1)} %param.21), kind=kOutput, calls=%fused_computation.3 | convolution fusion | flops 1207959552 | bytes 6881280 | tf_op jit(solution)/shard_map/dot_general | solution.py:94
  157.7 1.9 fusion.29
  159.6 1.9 fusion.26
  161.5 4.1 %convolution_convert_fusion = bf16[384,4096]{1,0:T(8,128)(2,1)} fusion(bf16[768,4096]{1,0:T(8,128)(2,1)S(1)} %bitcast.87, bf16[384,384]{0,1:T(8,128)(2,1)S(1)} %fusion.26, bf16[384,384]{0,1:T(8,128)(2,1)S(1)} %fusion.29), kind=kOutput, calls=%fused_computation | convolution fusion | flops 2418671616 | bytes 10027008 | tf_op jit(solution)/shard_map/dot_general | solution.py:98
  165.6 64.8 %reduce-scatter.5.cloned.1.call-done = bf16[24,4096]{1,0:T(8,128)(2,1)} async-done(((bf16[384,4096]{1,0:T(8,128)(2,1)}), bf16[24,4096]{1,0:T(8,128)(2,1)}) %reduce-scatter.5.cloned.1.call-update) | async-done | bytes 196624 | tf_op jit(solution)/shard_map/reduce_scatter | solution.py:103
  230.4 1.7 add_convert_fusion
  (45 shorter events, 0.5 us)
Async XLA Ops:
  6.5 65.0 %all-gather.3.cloned.1.call-start = ((), (), s32[]{:S(2)}) async-start(), calls=%async_computation.4 | async-start | bytes 3538944 | tf_op jit(solution)/shard_map/all_gather | solution.py:61
  12.8 3.5 %copy-start.3 = (bf16[48,4096]{1,0:T(8,128)(2,1)S(1)}, bf16[48,4096]{1,0:T(8,128)(2,1)}, u32[]{:S(2)}) copy-start(bf16[48,4096]{1,0:T(8,128)(2,1)} %param.12) | copy-start | bytes 1179652
  12.8 3.6 %copy-start.7 = (s32[48]{0:T(128)S(1)}, s32[48]{0:T(128)}, u32[]{:S(2)}) copy-start(s32[48]{0:T(128)} %param.15) | copy-start | bytes 580
  19.5 0.9 copy-start
  21.1 4.7 %copy-start.1 = (f32[48,2,16,128]{3,2,1,0:T(8,128)S(1)}, f32[48,2,16,128]{3,2,1,0:T(8,128)}, u32[]{:S(2)}) copy-start(f32[48,2,16,128]{3,2,1,0:T(8,128)} %copy-done) | copy-start | bytes 2359300
  30.5 65.5 %copy-start.4 = (bf16[4096]{0:T(1024)(128)(2,1)S(1)}, bf16[4096]{0:T(1024)(128)(2,1)}, u32[]{:S(2)}) copy-start(bf16[4096]{0:T(1024)(128)(2,1)} %param.18) | copy-start | bytes 24580
  30.5 59.1 %reduce-scatter.7.cloned.1.call-start = ((), (), s32[]{:S(2)}) async-start(), calls=%async_computation.7 | async-start | bytes 589824
  76.5 27.8 %copy-start.2 = (bf16[24,4096]{1,0:T(8,128)(2,1)S(1)}, bf16[24,4096]{1,0:T(8,128)(2,1)}, u32[]{:S(2)}) copy-start(bf16[24,4096]{1,0:T(8,128)(2,1)} %param.17) | copy-start | bytes 589828
  76.5 28.9 %copy-start.5 = (f32[48,8]{0,1:T(8,128)S(1)}, f32[48,8]{0,1:T(8,128)}, u32[]{:S(2)}) copy-start(f32[48,8]{0,1:T(8,128)} %param.20) | copy-start | bytes 4612
  76.5 28.9 %copy-start.6 = (s32[48,8]{0,1:T(8,128)S(1)}, s32[48,8]{0,1:T(8,128)}, u32[]{:S(2)}) copy-start(s32[48,8]{0,1:T(8,128)} %param.19) | copy-start | bytes 4612
  91.3 12.9 %all-to-all-start = ((bf16[8,24,512]{2,1,0:T(8,128)(2,1)}), bf16[8,24,512]{2,1,0:T(8,128)(2,1)S(1)}, u32[]{:S(2)}, u32[]{:S(2)}) async-start(bf16[8,24,512]{2,1,0:T(8,128)(2,1)} %copy.43), calls=%async_computation | async-start | bytes 393216 | tf_op jit(solution)/shard_map/all_to_all | solution.py:72
  95.9 52.9 %all-gather.5.cloned.1.call-start = ((), (), s32[]{:S(2)}) async-start(), calls=%async_computation.5 | async-start | bytes 3342336 | tf_op jit(solution)/shard_map/all_gather | solution.py:91
  105.3 125.0 %reduce-scatter.5.cloned.1.call-start = ((), (), s32[]{:S(2)}) async-start(), calls=%async_computation.6 | async-start | bytes 3342336 | tf_op jit(solution)/shard_map/reduce_scatter | solution.py:103
  148.9 4.8 %copy-start.8 = (bf16[384,4096]{1,0:T(8,128)(2,1)S(1)}, bf16[384,4096]{1,0:T(8,128)(2,1)}, u32[]{:S(2)}) copy-start(bf16[384,4096]{1,0:T(8,128)(2,1)} %all-gather.5.cloned.1.call-done) | copy-start | bytes 9437188
  148.9 8.8 %slice-start.2 = ((s8[6291456]{0:T(1024)(128)(4,1)}), s8[4194304]{0:T(1024)(128)(4,1)S(1)}, s32[]{:S(2)}) async-start(s8[6291456]{0:T(1024)(128)(4,1)} %bitcast.106), calls=%async_computation.10 | async-start | bytes 8388608
  153.7 3.9 %slice-start.3 = ((s8[6291456]{0:T(1024)(128)(4,1)}), s8[2097152]{0:T(1024)(128)(4,1)S(1)}, s32[]{:S(2)}) async-start(s8[6291456]{0:T(1024)(128)(4,1)} %bitcast.106), calls=%async_computation.11 | async-start | bytes 4194304
  157.7 3.8 %slice-start = ((s8[6291456]{0:T(1024)(128)(4,1)}), s8[4194304]{0:T(1024)(128)(4,1)S(1)}, s32[]{:S(2)}) async-start(s8[6291456]{0:T(1024)(128)(4,1)} %bitcast.85), calls=%async_computation.8 | async-start | bytes 8388608
  159.6 1.9 slice-start.1
Sparse Core Ops, SparseCore 0:
  30.6 40.9 all-gather.2
  77.5 12.0 reduce-scatter.6
  105.4 43.3 all-gather.4
  165.7 64.6 reduce-scatter.4

commit v2 on v1

--- a/solution.py
+++ b/solution.py
@@ -1,8 +1,11 @@
+import functools
 import math
 
 import jax
 import jax.numpy as jnp
 from jax import lax
+from jax.experimental import pallas as pl
+from jax.experimental.pallas import tpu as pltpu
 from jax.sharding import PartitionSpec as P
 
 HEAD_SIZE = 128
@@ -42,7 +45,515 @@
     return mixed.reshape(token_count, -1).astype(jnp.bfloat16)
 
 
-def per_device(
+CORES = 2
+MESH = pl.DeviceIdType.MESH
+DMA = pltpu.SemaphoreType.DMA
+VMEM_SPEC = pl.BlockSpec(memory_space=pltpu.VMEM)
+
+
+def remote(src, dst, send_sem, recv_sem, **device):
+    return pltpu.make_async_remote_copy(
+        src_ref=src,
+        dst_ref=dst,
+        send_sem=send_sem,
+        recv_sem=recv_sem,
+        device_id=device,
+        device_id_type=MESH,
+    )
+
+
+class Place:
+    def __init__(self, chips, groups):
+        self.chips, self.groups = chips, groups
+        self.expert = lax.axis_index("expert")
+        self.tensor = lax.axis_index("tensor")
+        self.chip, self.core = self.expert // CORES, self.expert % CORES
+        self.partner = self.chip * CORES + 1 - self.core
+
+    def inside(self, chip):
+        return jnp.logical_and(chip >= 0, chip < self.chips)
+
+    def greet_line(self, barrier):
+        pl.semaphore_signal(barrier, 1, device_id={"expert": self.partner}, device_id_type=MESH)
+        for step in (-1, 1):
+
+            @pl.when(self.inside(self.chip + step))
+            def _():
+                pl.semaphore_signal(
+                    barrier,
+                    1,
+                    device_id={"expert": self.expert + CORES * step},
+                    device_id_type=MESH,
+                )
+
+        ends = (self.chip == 0).astype(jnp.int32) + (self.chip == self.chips - 1).astype(jnp.int32)
+        return 3 - ends
+
+    def greet_tensor(self, barrier):
+        for shift in range(1, self.groups):
+            other = (self.tensor + shift) % self.groups
+            pl.semaphore_signal(barrier, 1, device_id={"tensor": other}, device_id_type=MESH)
+        return self.groups - 1
+
+
+def line_gather(place, arrays, sems, slot, across):
+    line_send, line_recv, core_send, core_recv, cross_send, cross_recv = sems
+    chips, core = place.chips, place.core
+    groups = place.groups if across else 1
+    waits = []
+
+    def block(a, chip, tensor, own):
+        source, whole = arrays[a]
+        if own:
+            return source
+        return whole.at[slot(chip * CORES + core, tensor)]
+
+    def landing(a, chip, tensor, of_core):
+        return arrays[a][1].at[slot(chip * CORES + of_core, tensor)]
+
+    def line(a, side, step, chip, own):
+        way = 1 - 2 * side
+        return remote(
+            block(a, chip, place.tensor, own),
+            landing(a, chip, place.tensor, core),
+            line_send.at[a, side, step],
+            line_recv.at[a, side, step + 1],
+            expert=place.expert + CORES * way,
+        )
+
+    def line_arrival(a, side, step, chip):
+        here = landing(a, chip, place.tensor, core)
+        return remote(here, here, line_send.at[a, side, step], line_recv.at[a, side, step],
+                      expert=place.partner)
+
+    def to_partner(a, shift, chip, own):
+        tensor = (place.tensor + shift) % place.groups
+        return remote(
+            block(a, chip, tensor, own),
+            landing(a, chip, tensor, core),
+            core_send.at[a, shift, chip],
+            core_recv.at[a, shift, chip],
+            expert=place.partner,
+        )
+
+    def partner_arrival(a, shift, chip):
+        tensor = (place.tensor + shift) % place.groups
+        here = landing(a, chip, tensor, 1 - core)
+        return remote(here, here, core_send.at[a, shift, chip], core_recv.at[a, shift, chip],
+                      expert=place.partner)
+
+    def cross(a, shift, chip, own):
+        other = (place.tensor + shift) % place.groups
+        return remote(
+            block(a, chip, place.tensor, own),
+            landing(a, chip, place.tensor, core),
+            cross_send.at[a, shift, chip],
+            cross_recv.at[a, shift, chip],
+            tensor=other,
+        )
+
+    def cross_arrival(a, shift, chip):
+        tensor = (place.tensor + place.groups - shift) % place.groups
+        here = landing(a, chip, tensor, core)
+        return remote(here, here, cross_send.at[a, shift, chip], cross_recv.at[a, shift, chip],
+                      expert=place.partner)
+
+    count = len(arrays)
+
+    def hand_on(step, side, chip):
+        own = step == 0
+        way = 1 - 2 * side
+
+        @pl.when(place.inside(chip))
+        def _():
+            if not own:
+                for a in range(count):
+                    line_arrival(a, side, step, chip).wait_recv()
+
+            @pl.when(place.inside(place.chip + way))
+            def _():
+                for a in range(count):
+                    line(a, side, step, chip, own).start()
+
+            if not own or side == 0:
+                for a in range(count):
+                    for shift in range(1, groups):
+                        cross(a, shift, chip, own).start()
+                    to_partner(a, 0, chip, own).start()
+
+    def hand_on_crossed(step, side, chip):
+        if step == 0 and side == 1:
+            return
+
+        @pl.when(place.inside(chip))
+        def _():
+            for a in range(count):
+                for shift in range(1, groups):
+                    cross_arrival(a, shift, chip).wait_recv()
+                    to_partner(a, place.groups - shift, chip, False).start()
+
+    sides = [(side, step) for step in range(chips) for side in range(2)]
+    chip_at = lambda side, step: place.chip - (1 - 2 * side) * step
+    for step in range(chips):
+        for side in range(2):
+            hand_on(step, side, chip_at(side, step))
+        if step > 0 and groups > 1:
+            for side in range(2):
+                hand_on_crossed(step - 1, side, chip_at(side, step - 1))
+    if groups > 1:
+        for side in range(2):
+            hand_on_crossed(chips - 1, side, chip_at(side, chips - 1))
+    for chip in range(chips):
+        for shift in range(groups):
+            for a in range(count):
+                partner_arrival(a, shift, chip).wait_recv()
+    for side, step in sides:
+        own = step == 0
+        chip = chip_at(side, step)
+
+        @pl.when(jnp.logical_and(place.inside(chip), place.inside(place.chip + 1 - 2 * side)))
+        def _():
+            for a in range(count):
+                line(a, side, step, chip, own).wait_send()
+
+    for a in range(count):
+        for shift in range(groups):
+            for chip in range(chips):
+                partner_arrival(a, shift, chip).wait_send()
+                if shift:
+                    cross_arrival(a, shift, chip).wait_send()
+
+
+def gather_sems(count, chips, groups):
+    return [
+        DMA((count, 2, chips)),
+        DMA((count, 2, chips + 1)),
+        DMA((count, groups, chips)),
+        DMA((count, groups, chips)),
+        DMA((count, groups, chips)),
+        DMA((count, groups, chips)),
+    ]
+
+
+def attended_kernel(chips, groups, rows, weights, all_rows, all_weights, own_sem, *sems):
+    place = Place(chips, groups)
+    barrier = pltpu.get_barrier_semaphore()
+    pl.semaphore_wait(barrier, place.greet_line(barrier))
+    keep = [
+        pltpu.make_async_copy(rows, all_rows.at[place.expert], own_sem.at[0]),
+        pltpu.make_async_copy(weights, all_weights.at[place.expert], own_sem.at[1]),
+    ]
+    for copy in keep:
+        copy.start()
+    line_gather(
+        place,
+        [(rows, all_rows), (weights, all_weights)],
+        sems,
+        lambda expert, tensor: expert,
+        False,
+    )
+    for copy in keep:
+        copy.wait()
+
+
+def gather_attended(rows, weights, groups):
+    experts = lax.axis_size("expert")
+    chips = experts // CORES
+    return pl.pallas_call(
+        functools.partial(attended_kernel, chips, groups),
+        out_shape=[
+            jax.ShapeDtypeStruct((experts,) + rows.shape, rows.dtype),
+            jax.ShapeDtypeStruct((experts,) + weights.shape, weights.dtype),
+        ],
+        in_specs=[VMEM_SPEC] * 2,
+        out_specs=[VMEM_SPEC] * 2,
+        scratch_shapes=[DMA((2,))] + gather_sems(2, chips, groups),
+        compiler_params=pltpu.CompilerParams(collective_id=0, has_side_effects=True),
+    )(rows, weights)
+
+
+def stream_kernel(
+    chips, groups, projected, residual, gain, stream, normed, own, crossed, summed, arrived,
+    swap_send, swap_recv, out_send, out_recv, *sems
+):
+    place = Place(chips, groups)
+    experts = chips * CORES
+    barrier = pltpu.get_barrier_semaphore()
+    for shift in range(1, experts):
+        other = (place.expert + shift) % experts
+        pl.semaphore_signal(barrier, 1, device_id={"expert": other}, device_id_type=MESH)
+    pl.semaphore_wait(barrier, experts - 1 + place.greet_tensor(barrier))
+
+    def swap(shift):
+        other = (place.tensor + shift) % groups
+        return remote(
+            projected.at[other],
+            crossed.at[shift - 1],
+            swap_send.at[shift - 1],
+            swap_recv.at[shift - 1],
+            tensor=other,
+        )
+
+    def hand_out(shift):
+        other = (place.expert + shift) % experts
+        return remote(
+            summed.at[other],
+            arrived.at[shift],
+            out_send.at[shift],
+            out_recv.at[shift],
+            expert=other,
+        )
+
+    for shift in range(1, groups):
+        swap(shift).start()
+    for shift in range(1, groups):
+        swap(shift).wait()
+    for shift in list(range(1, experts)) + [0]:
+        expert = (place.expert + shift) % experts
+        total = projected[place.tensor, expert].astype(jnp.float32)
+        for other in range(groups - 1):
+            total = total + crossed[other, expert].astype(jnp.float32)
+        summed[expert] = total.astype(jnp.bfloat16)
+        if shift:
+            hand_out(shift).start()
+    for shift in range(1, experts):
+        hand_out(shift).wait()
+    arrived[0] = summed[place.expert]
+    width = stream.shape[1] // experts
+    square = 0.0
+    for expert in range(experts):
+        columns = pl.ds(expert * width, width)
+        shift = (place.expert - expert + experts) % experts
+        part = residual[:, columns].astype(jnp.float32) + arrived[shift].astype(jnp.float32)
+        stream[:, columns] = part
+        square = square + jnp.sum(part * part, axis=1, keepdims=True)
+    scale = lax.rsqrt(square * (1.0 / stream.shape[1]) + 1e-06)
+    for expert in range(experts):
+        columns = pl.ds(expert * width, width)
+        value = stream[:, columns] * scale * gain[:, columns].astype(jnp.float32)
+        own[:, columns] = value.astype(jnp.bfloat16)
+    mine = place.expert * groups + place.tensor
+    normed[mine] = own[...]
+    line_gather(
+        place, [(own, normed)], sems, lambda expert, tensor: expert * groups + tensor, True
+    )
+
+
+def exchange_stream(projected, residual, gain):
+    groups, experts, rows, width = projected.shape
+    chips = experts // CORES
+    model = residual.shape[1]
+    return pl.pallas_call(
+        functools.partial(stream_kernel, chips, groups),
+        out_shape=[
+            jax.ShapeDtypeStruct((rows, model), jnp.float32),
+            jax.ShapeDtypeStruct((experts * groups, rows, model), jnp.bfloat16),
+        ],
+        in_specs=[VMEM_SPEC] * 3,
+        out_specs=[VMEM_SPEC] * 2,
+        scratch_shapes=[
+            pltpu.VMEM((rows, model), jnp.bfloat16),
+            pltpu.VMEM((max(groups - 1, 1), experts, rows, width), jnp.bfloat16),
+            pltpu.VMEM((experts, rows, width), jnp.bfloat16),
+            pltpu.VMEM((experts, rows, width), jnp.bfloat16),
+            DMA((groups,)),
+            DMA((groups,)),
+            DMA((experts,)),
+            DMA((experts,)),
+        ]
+        + gather_sems(1, chips, groups),
+        compiler_params=pltpu.CompilerParams(collective_id=1, has_side_effects=True),
+    )(projected, residual, gain)
+
+
+def scatter_kernel(
+    chips, groups, partial, total, core_in, crossing, cross_in, sums, line_in,
+    core_send, core_recv, cross_send, cross_recv, line_send, line_recv
+):
+    place = Place(chips, groups)
+    chip, core, tensor = place.chip, place.core, place.tensor
+    barrier = pltpu.get_barrier_semaphore()
+    peers = place.greet_line(barrier) + place.greet_tensor(barrier)
+    pl.semaphore_wait(barrier, peers)
+
+    def target(m):
+        low = jnp.where(m < chips - 1 - chip, chips - 1 - m, m - (chips - 1 - chip))
+        high = jnp.where(m < chip, m, chips - 1 - (m - chip))
+        return jnp.where(chip * 2 < chips, low, high)
+
+    def to_partner(m, shift):
+        j, t = target(m), (tensor + shift) % groups
+        return remote(
+            partial.at[(j * CORES + 1 - core) * groups + t],
+            core_in.at[j * groups + t],
+            core_send.at[m, shift],
+            core_recv.at[m, shift],
+            expert=place.partner,
+        )
+
+    def cross(m, shift):
+        j = target(m)
+        return remote(
+            crossing.at[shift - 1, j],
+            cross_in.at[shift - 1, j],
+            cross_send.at[m, shift],
+            cross_recv.at[m, shift],
+            tensor=(tensor + shift) % groups,
+        )
+
+    def pair_sum(m, shift):
+        j, t = target(m), (tensor + shift) % groups
+        mine = partial[(j * CORES + core) * groups + t].astype(jnp.float32)
+        return mine + core_in[j * groups + t].astype(jnp.float32)
+
+    for shift in list(range(1, groups)) + [0]:
+        for m in range(chips):
+            to_partner(m, shift).start()
+    for m in range(chips):
+        for shift in range(1, groups):
+            to_partner(m, shift).wait_recv()
+            crossing[shift - 1, target(m)] = pair_sum(m, shift).astype(jnp.bfloat16)
+            cross(m, shift).start()
+
+    def along(j, side):
+        way = 1 - 2 * side
+        return remote(
+            sums.at[j],
+            line_in.at[side, j],
+            line_send.at[j],
+            line_recv.at[side, j],
+            expert=place.expert + CORES * way,
+        )
+
+    def line_arrival(j, side):
+        return remote(line_in.at[side, j], line_in.at[side, j], line_send.at[j],
+                      line_recv.at[side, j], expert=place.partner)
+
+    for m in range(chips):
+        j = target(m)
+        to_partner(m, 0).wait_recv()
+        value = pair_sum(m, 0)
+        for shift in range(1, groups):
+            cross(m, shift).wait_recv()
+            value = value + cross_in[shift - 1, j].astype(jnp.float32)
+        if m < chips - 1:
+            for side in range(2):
+                ahead = j > chip if side == 0 else j < chip
+                source = place.inside(chip - (1 - 2 * side))
+
+                @pl.when(jnp.logical_and(ahead, source))
+                def _():
+                    line_arrival(j, side).wait_recv()
+                    sums[j] = (value + line_in[side, j].astype(jnp.float32)).astype(jnp.bfloat16)
+                    along(j, side).start()
+
+                @pl.when(jnp.logical_and(ahead, jnp.logical_not(source)))
+                def _():
+                    sums[j] = value.astype(jnp.bfloat16)
+                    along(j, side).start()
+
+        else:
+            total[...] = value
+            for side in range(2):
+
+                @pl.when(place.inside(chip - (1 - 2 * side)))
+                def _():
+                    line_arrival(j, side).wait_recv()
+                    total[...] += line_in[side, j].astype(jnp.float32)
+
+    for m in range(chips):
+        for shift in range(groups):
+            to_partner(m, shift).wait_send()
+            if shift:
+                cross(m, shift).wait_send()
+        if m < chips - 1:
+            line_arrival(target(m), 0).wait_send()
+
+
+def scatter_sum(partial, groups):
+    blocks, rows, model = partial.shape
+    experts = blocks // groups
+    chips = experts // CORES
+    block = (rows, model)
+    others = max(groups - 1, 1)
+    return pl.pallas_call(
+        functools.partial(scatter_kernel, chips, groups),
+        out_shape=jax.ShapeDtypeStruct(block, jnp.float32),
+        in_specs=[VMEM_SPEC],
+        out_specs=VMEM_SPEC,
+        scratch_shapes=[
+            pltpu.VMEM((chips * groups,) + block, jnp.bfloat16),
+            pltpu.VMEM((others, chips) + block, jnp.bfloat16),
+            pltpu.VMEM((others, chips) + block, jnp.bfloat16),
+            pltpu.VMEM((chips,) + block, jnp.bfloat16),
+            pltpu.VMEM((2, chips) + block, jnp.bfloat16),
+        ]
+        + [DMA((chips, groups))] * 4
+        + [DMA((chips,)), DMA((2, chips))],
+        compiler_params=pltpu.CompilerParams(collective_id=2, has_side_effects=True),
+    )(partial)
+
+
+def route_table(expert_ids, route_weights, expert_total):
+    named = expert_ids[:, :, None] == jnp.arange(expert_total, dtype=jnp.int32)[None, None, :]
+    return jnp.sum(jnp.where(named, route_weights[:, :, None], 0.0), axis=1)
+
+
+def experts_sum(whole_rows, mixing, w_gate, w_up, w_down):
+    pieces = []
+    for x in range(w_gate.shape[0]):
+        gate_proj = jnp.dot(whole_rows, w_gate[x], preferred_element_type=jnp.float32)
+        up_proj = jnp.dot(whole_rows, w_up[x], preferred_element_type=jnp.float32)
+        activated = jax.nn.silu(gate_proj) * up_proj * mixing[:, x][:, None]
+        pieces.append(activated.astype(jnp.bfloat16))
+    return jnp.dot(
+        jnp.concatenate(pieces, axis=1),
+        w_down.reshape(-1, w_down.shape[2]),
+        preferred_element_type=jnp.float32,
+    ).astype(jnp.bfloat16)
+
+
+def with_kernels(
+    query,
+    latest_key_value,
+    cache,
+    lengths,
+    w_out,
+    residual_in,
+    norm_gain,
+    expert_ids,
+    route_weights,
+    w_gate,
+    w_up,
+    w_down,
+):
+    experts, groups = lax.axis_size("expert"), lax.axis_size("tensor")
+    local_experts = w_gate.shape[0]
+    expert_total = local_experts * experts
+    rows, model = residual_in.shape
+    table = route_table(expert_ids, route_weights, expert_total)
+    high = table.astype(jnp.bfloat16)
+    low = (table - high.astype(jnp.float32)).astype(jnp.bfloat16)
+    pair = jnp.concatenate([high, low], axis=1)
+    pair = jnp.pad(pair, ((0, 0), (0, -pair.shape[1] % 128)))
+    attended = attention(query, latest_key_value, cache, lengths)
+    all_attended, all_pairs = gather_attended(attended, pair, groups)
+    all_pairs = all_pairs.reshape(-1, pair.shape[1]).astype(jnp.float32)
+    tables = all_pairs[:, :expert_total] + all_pairs[:, expert_total : 2 * expert_total]
+    mixing = lax.dynamic_slice_in_dim(
+        tables, lax.axis_index("expert") * local_experts, local_experts, axis=1
+    )
+    projected = jnp.dot(
+        all_attended.reshape(-1, attended.shape[1]), w_out, preferred_element_type=jnp.float32
+    ).astype(jnp.bfloat16)
+    projected = projected.reshape(experts, groups, rows, -1).swapaxes(0, 1)
+    stream, normed = exchange_stream(projected, residual_in, norm_gain.reshape(1, model))
+    partial_out = experts_sum(normed.reshape(-1, model), mixing, w_gate, w_up, w_down)
+    mixture = scatter_sum(partial_out.reshape(experts * groups, rows, model), groups)
+    return (stream + mixture).astype(jnp.bfloat16)
+
+
+def with_collectives(
     query,
     latest_key_value,
     cache,
@@ -121,6 +632,13 @@
         P("expert", None, "tensor"),
         P("expert", "tensor", None),
     )
+
+    def per_device(*arrays):
+        rows, columns = arrays[5].shape[0], arrays[4].shape[1]
+        whole_tiles = rows % 8 == 0 and columns % 128 == 0
+        paired = mesh.shape["expert"] % CORES == 0
+        return (with_kernels if whole_tiles and paired else with_collectives)(*arrays)
+
     return jax.shard_map(
         per_device,
         mesh=mesh,

time: 239 us -> 157 us (0.66)
  waiting for transfers between devices: 162 us -> 0 us
  Pallas kernels: 0 us -> 107 us
  between operations: 13.4 us -> 0.39 us
  blocking collectives: 7.98 us -> 0 us
  starting transfers between devices: 4.74 us -> 0 us
    pallas_call x0 -> x3, Pallas kernels: none -> 107 us  [the longest x1 39.9 us: exchange_stream(): pl.pallas_call(functools.partial(stream_kernel, chips, groups), out_shape...]
    all_gather x2 -> x0, waiting for transfers between devices: 76.4 us -> none  [the longest x1 41 us: per_device(): lax.all_gather(attended, 'expert', axis=0, tiled=True)]
    reduce_scatter x1 -> x0, waiting for transfers between devices: 64.8 us -> none  [per_device(): lax.psum_scatter(partial_out.astype(jnp.bfloat16), ('expert', 'tensor'),...]
    unnamed x5 -> x0, waiting for transfers between devices: 12.3 us -> none
    all_to_all x1 -> x0, waiting for transfers between devices: 8.24 us -> none  [per_device(): lax.all_to_all(summed.astype(jnp.bfloat16), 'expert', split_axis=0, conca...]
    all_to_all x1 -> x0, blocking collectives: 7.98 us -> none  [per_device(): lax.all_to_all(mixing.reshape(token_count, expert_groups, local_experts),...]
    all_to_all x1 -> x0, starting transfers between devices: 4.62 us -> none  [per_device(): lax.all_to_all(summed.astype(jnp.bfloat16), 'expert', split_axis=0, conca...]
    unnamed x34 -> x40, local copies, waits for them, and re-layouts: 12.7 us -> 10.1 us
  transfers between devices with their start and end apart: 5 -> 0, of which waited for: 5 -> 0; matrix products, arithmetic and copies ran while one was open for 0% -> 0% of each run, Pallas kernels for 0% -> 0%
where the time goes in v2:
time: 157 us
  Pallas kernels  107 us (68%)
  matrix products  26.7 us (17%)
  local copies, waits for them, and re-layouts  18.2 us (12%)
  other arithmetic  4.18 us (3%)
    pallas_call x1, Pallas kernels, exchange_stream(): pl.pallas_call(functools.partial(stream_kernel, chips, groups), out_shape...  39.9 us
    pallas_call x1, Pallas kernels, gather_attended(): pl.pallas_call(functools.partial(attended_kernel, chips, groups), out_sha...  38.9 us
    pallas_call x1, Pallas kernels, scatter_sum(): pl.pallas_call(functools.partial(scatter_kernel, chips, groups), out_shap...  28.4 us
    unnamed x40, local copies, waits for them, and re-layouts  10.1 us
    dot_general x2, matrix products, experts_sum(): jnp.dot(whole_rows, w_gate[x], preferred_element_type=jnp.float32)  6.64 us
    slice x1, local copies, waits for them, and re-layouts, attention(): cache[:, 0].reshape(token_count, positions, kv_heads, HEAD_SIZE)  6.25 us
    dot_general x2, matrix products, experts_sum(): up_proj = jnp.dot(whole_rows, w_up[x], preferred_element_type=jnp.float32)  5.97 us
    dot_general x1, matrix products, with_kernels(): jnp.dot(all_attended.reshape(-1, attended.shape[1]), w_out, preferred_ele...  4.93 us

profile of v2, /device:TPU:0, one launch (start us, length us, event | category | flops | bytes accessed | tf_op | source)
XLA Modules:
  0.0 156.7 jit_solution(16088633319036949214)
XLA Ops:
  0.0 6.2 %fusion.46 = (bf16[48,1,128,256]{3,2,1,0:T(8,128)(2,1)}, bf16[48,1,128,256]{3,2,1,0:T(8,128)(2,1)}) fusion(bf16[48,2,128,256]{3,2,1,0:T(8,128)(2,1)} %param.14), kind=kLoop, calls=%fused_computation.57 | loop fusion | bytes 12582912 | tf_op jit(solution)/shard_map/slice | solution.py:21
  6.3 3.5 %copy.47 = bf16[48,1,128,256]{2,3,0,1:T(8,128)(2,1)S(1)} copy(bf16[48,1,128,256]{3,2,1,0:T(8,128)(2,1)} %get-tuple-element.15) | data formatting | bytes 6291456
  9.8 0.1 copy.53
  9.9 0.1 iota_compare_fusion.2
  10.0 1.1 fusion.48
  11.1 0.3 fusion.38
  11.4 0.5 copy-done
  12.0 0.6 fusion.32
  12.5 0.1 fusion.45
  12.7 4.7 %copy.48 = bf16[48,1,128,256]{2,3,0,1:T(8,128)(2,1)} copy(bf16[48,1,128,256]{3,2,1,0:T(8,128)(2,1)} %get-tuple-element.16) | data formatting | bytes 6291456
  17.5 3.7 %fusion.13 = bf16[48,2,16,128]{3,2,1,0:T(8,128)(2,1)S(1)} fusion(bf16[48,128,2,128]{1,3,2,0:T(8,128)(2,1)} %bitcast.67, f32[48,2,16,128]{3,2,1,0:T(8,128)S(1)} %copy-done.1, f32[48,2,128]{2,1,0:T(2,128)S(1)} %bitcast.77, f32[48,2,16]{2,1,0:T(2,128)S(1)} %convert_element_type.58, f32[48,2,16]{2,1,0:T(2,128)S(1)} %get-tuple-element.19, ...), kind=kOutput, calls=%fused_computation.16 | convolution fusion | flops 51511296 | bytes 4392960 | tf_op jit(solution)/shard_map/tkgl,tlkd->tkgd/dot_general | solution.py:43
  21.2 0.9 copy.57
  22.2 0.1 copy.39
  22.3 0.1 copy.38
  22.4 0.7 fusion.43.weights
  23.0 38.9 %shard_map.118 = (bf16[8,48,4096]{2,1,0:T(8,128)(2,1)}, bf16[8,48,128]{2,1,0:T(8,128)(2,1)}) custom-call(bf16[48,4096]{1,0:T(8,128)(2,1)} %bitcast.68, bf16[48,128]{1,0:T(8,128)(2,1)} %fusion.43.weights), custom_call_target="tpu_custom_call" | custom-call | tf_op jit(solution)/shard_map/pallas_call | solution.py:262
  61.9 0.9 bitcast_convert_fusion
  62.8 0.1 fusion.47
  63.0 0.2 constant_dynamic-slice_fusion
  63.1 0.1 copy.51
  63.2 0.1 copy.52
  63.4 4.9 %convolution_convert_fusion.1 = bf16[384,512]{1,0:T(8,128)(2,1)S(1)} fusion(bf16[384,4096]{1,0:T(8,128)(2,1)} %bitcast.82, bf16[4096,512]{1,0:T(8,128)(2,1)} %param.16), kind=kOutput, calls=%fused_computation.21 | convolution fusion | flops 1610809344 | bytes 7733248 | tf_op jit(solution)/shard_map/dot_general | solution.py:546
  68.3 0.8 copy.58
  69.1 0.6 reshape.58.gain
  69.8 39.9 %shard_map.119 = (f32[24,4096]{1,0:T(8,128)}, bf16[16,24,4096]{2,1,0:T(8,128)(2,1)}) custom-call(bf16[2,8,24,512]{3,2,1,0:T(8,128)(2,1)} %bitcast.71, bf16[24,4096]{1,0:T(8,128)(2,1)} %residual.1, bf16[1,4096]{1,0:T(2,128)(2,1)} %reshape.58.gain), custom_call_target="tpu_custom_call" | custom-call | tf_op jit(solution)/shard_map/pallas_call | solution.py:346
  109.7 4.8 %fusion.6 = f32[384,384]{0,1:T(8,128)S(1)} fusion(bf16[384,4096]{1,0:T(8,128)(2,1)} %bitcast.83, bf16[2,4096,384]{2,1,0:T(8,128)(2,1)} %param.21), kind=kOutput, calls=%fused_computation.7 | convolution fusion | flops 1207959552 | bytes 6881280 | tf_op jit(solution)/shard_map/dot_general | solution.py:505
  114.6 4.1 %fusion.29 = bf16[384,384]{0,1:T(8,128)(2,1)S(1)} fusion(bf16[384,4096]{1,0:T(8,128)(2,1)S(1)} %bitcast.84, bf16[2,4096,384]{2,1,0:T(8,128)(2,1)} %param.22, f32[384,384]{0,1:T(8,128)S(1)} %fusion.6, f32[384]{0:T(512)S(1)} %get-tuple-element.13), kind=kOutput, calls=%fused_computation.23 | convolution fusion | flops 1208991744 | bytes 7177728 | tf_op jit(solution)/shard_map/dot_general | solution.py:506
  118.7 1.8 %fusion.2 = f32[384,384]{0,1:T(8,128)S(1)} fusion(bf16[384,4096]{1,0:T(8,128)(2,1)S(1)} %bitcast.85, bf16[2,4096,384]{2,1,0:T(8,128)(2,1)S(1)} %bitcast.79), kind=kOutput, calls=%fused_computation.3 | convolution fusion | flops 1207959552 | bytes 6881280 | tf_op jit(solution)/shard_map/dot_general | solution.py:505
  120.6 1.9 %fusion.26 = bf16[384,384]{0,1:T(8,128)(2,1)S(1)} fusion(bf16[384,4096]{1,0:T(8,128)(2,1)S(1)} %bitcast.86, bf16[2,4096,384]{2,1,0:T(8,128)(2,1)S(1)} %bitcast.81, f32[384,384]{0,1:T(8,128)S(1)} %fusion.2, f32[384]{0:T(512)S(1)} %get-tuple-element.14), kind=kOutput, calls=%fused_computation.22 | convolution fusion | flops 1208991744 | bytes 7178240 | tf_op jit(solution)/shard_map/dot_general | solution.py:506
  122.5 4.1 %convolution_convert_fusion = bf16[384,4096]{1,0:T(8,128)(2,1)} fusion(bf16[768,4096]{1,0:T(8,128)(2,1)S(1)} %bitcast.66, bf16[384,384]{0,1:T(8,128)(2,1)S(1)} %fusion.26, bf16[384,384]{0,1:T(8,128)(2,1)S(1)} %fusion.29), kind=kOutput, calls=%fused_computation | convolution fusion | flops 2418671616 | bytes 10027008 | tf_op jit(solution)/shard_map/dot_general | solution.py:509
  126.6 28.4 %shard_map.120 = f32[24,4096]{1,0:T(8,128)} custom-call(bf16[16,24,4096]{2,1,0:T(8,128)(2,1)} %bitcast.63), custom_call_target="tpu_custom_call" | custom-call | tf_op jit(solution)/shard_map/pallas_call | solution.py:479
  155.0 1.7 %add_convert_fusion = bf16[24,4096]{1,0:T(8,128)(2,1)} fusion(f32[24,4096]{1,0:T(8,128)S(1)} %copy-done.3, f32[24,4096]{1,0:T(8,128)} %shard_map.120), kind=kLoop, calls=%fused_computation.32 | loop fusion | flops 196608 | bytes 983040 | tf_op jit(solution)/shard_map/convert_element_type | solution.py:553
  (44 shorter events, 0.3 us)
Async XLA Ops:
  6.2 3.6 %copy-start.2 = (bf16[48,4096]{1,0:T(8,128)(2,1)S(1)}, bf16[48,4096]{1,0:T(8,128)(2,1)}, u32[]{:S(2)}) copy-start(bf16[48,4096]{1,0:T(8,128)(2,1)} %param.12) | copy-start | bytes 1179652
  6.2 3.6 %copy-start.9 = (s32[48]{0:T(128)S(1)}, s32[48]{0:T(128)}, u32[]{:S(2)}) copy-start(s32[48]{0:T(128)} %param.15) | copy-start | bytes 580
  9.8 1.3 copy-start.4
  11.0 0.9 copy-start
  12.6 4.8 %copy-start.5 = (bf16[48,2,256]{2,1,0:T(2,128)(2,1)S(1)}, bf16[48,2,256]{2,1,0:T(2,128)(2,1)}, u32[]{:S(2)}) copy-start(bf16[48,2,256]{2,1,0:T(2,128)(2,1)} %param.13) | copy-start | bytes 147460
  12.7 4.8 %copy-start.1 = (f32[48,2,16,128]{3,2,1,0:T(8,128)S(1)}, f32[48,2,16,128]{3,2,1,0:T(8,128)}, u32[]{:S(2)}) copy-start(f32[48,2,16,128]{3,2,1,0:T(8,128)} %copy-done) | copy-start | bytes 2359300
  17.5 4.6 %copy-start.7 = (f32[48,8]{0,1:T(8,128)S(1)}, f32[48,8]{0,1:T(8,128)}, u32[]{:S(2)}) copy-start(f32[48,8]{0,1:T(8,128)} %param.20) | copy-start | bytes 4612
  17.5 4.6 %copy-start.8 = (s32[48,8]{0,1:T(8,128)S(1)}, s32[48,8]{0,1:T(8,128)}, u32[]{:S(2)}) copy-start(s32[48,8]{0,1:T(8,128)} %param.19) | copy-start | bytes 4612
  63.4 5.7 %copy-start.6 = (bf16[4096]{0:T(1024)(128)(2,1)S(1)}, bf16[4096]{0:T(1024)(128)(2,1)}, u32[]{:S(2)}) copy-start(bf16[4096]{0:T(1024)(128)(2,1)} %param.18) | copy-start | bytes 24580
  109.7 4.9 %copy-start.10 = (bf16[16,24,4096]{2,1,0:T(8,128)(2,1)S(1)}, bf16[16,24,4096]{2,1,0:T(8,128)(2,1)}, u32[]{:S(2)}) copy-start(bf16[16,24,4096]{2,1,0:T(8,128)(2,1)} %get-tuple-element.11) | copy-start | bytes 9437188
  109.7 9.0 %slice-start.2 = ((s8[6291456]{0:T(1024)(128)(4,1)}), s8[4194304]{0:T(1024)(128)(4,1)S(1)}, s32[]{:S(2)}) async-start(s8[6291456]{0:T(1024)(128)(4,1)} %bitcast.78), calls=%async_computation.2 | async-start | bytes 8388608
  109.7 10.9 %slice-start.4 = ((s8[6291456]{0:T(1024)(128)(4,1)}), s8[4194304]{0:T(1024)(128)(4,1)S(1)}, s32[]{:S(2)}) async-start(s8[6291456]{0:T(1024)(128)(4,1)} %bitcast.80), calls=%async_computation.4 | async-start | bytes 8388608
  114.5 4.2 %slice-start.3 = ((s8[6291456]{0:T(1024)(128)(4,1)}), s8[2097152]{0:T(1024)(128)(4,1)S(1)}, s32[]{:S(2)}) async-start(s8[6291456]{0:T(1024)(128)(4,1)} %bitcast.78), calls=%async_computation.3 | async-start | bytes 4194304
  114.6 6.0 %slice-start.5 = ((s8[6291456]{0:T(1024)(128)(4,1)}), s8[2097152]{0:T(1024)(128)(4,1)S(1)}, s32[]{:S(2)}) async-start(s8[6291456]{0:T(1024)(128)(4,1)} %bitcast.80), calls=%async_computation.5 | async-start | bytes 4194304
  118.7 3.8 %slice-start = ((s8[6291456]{0:T(1024)(128)(4,1)}), s8[4194304]{0:T(1024)(128)(4,1)S(1)}, s32[]{:S(2)}) async-start(s8[6291456]{0:T(1024)(128)(4,1)} %bitcast.64), calls=%async_computation | async-start | bytes 8388608
  120.6 1.9 %slice-start.1 = ((s8[6291456]{0:T(1024)(128)(4,1)}), s8[2097152]{0:T(1024)(128)(4,1)S(1)}, s32[]{:S(2)}) async-start(s8[6291456]{0:T(1024)(128)(4,1)} %bitcast.64), calls=%async_computation.1 | async-start | bytes 4194304
  126.6 28.4 %copy-start.3 = (f32[24,4096]{1,0:T(8,128)S(1)}, f32[24,4096]{1,0:T(8,128)}, u32[]{:S(2)}) copy-start(f32[24,4096]{1,0:T(8,128)} %get-tuple-element.10) | copy-start | bytes 1179652
